TPU v7x, 256 devices: a whole 4x4x8 slice. The times are simulated.
256 devices in a mesh: rep: 16 (over x_hi, z), atom: 16 (over x_lo, y, core).
Axes of the slice: x: 4 (x_hi: 2, x_lo: 2; x = x_hi * 2 + x_lo), y: 4, z: 8, core: 2. Of those that a mesh axis runs over, the one named last changes fastest.
Arguments:
- starting_locations: float32 [64, 3, 16384], P('rep', None, 'atom'), may hold values from 0 to 16
- starting_speeds: float32 [64, 3, 16384], P('rep', None, 'atom'), may hold values from -5 to 5
- terminal_location_adjoint: float32 [64, 3, 16384], P('rep', None, 'atom'), may hold values from -6 to 6
- terminal_speed_adjoint: float32 [64, 3, 16384], P('rep', None, 'atom'), may hold values from -7.5 to 7.5
- interaction_strength: float32 [16384], P('atom'), may hold values from 0.5 to 2
- reciprocal_particle_weight: float32 [16384], P('atom'), may hold values from 0.05 to 2
- heat_levels: float32 [64], P('rep'), may hold values from 0.25 to 4
- swap_indicator: int32 [64], P('rep'), may hold values from 0 to 1, as said below
- companion_group_indices: int32 [5, 128, 2], P(None, 'atom'), may hold values from 0 to 23, as said below
Outputs:
- final_pos: float32 [64, 3, 16384], P('rep', None, 'atom')
- final_vel: float32 [64, 3, 16384], P('rep', None, 'atom')
- energies: float32 [64], P('rep')
- grad_pos: float32 [64, 3, 16384], P('rep', None, 'atom')
- grad_vel: float32 [64, 3, 16384], P('rep', None, 'atom')
- grad_coupling: float32 [16384], P('atom')
Inputs may be any that keep to these rules, and one draw needn't show every extreme that they name: `swap_indicator`: replicas r and r + 4, for r with r // 4 even, carry the same flag; among the replicas r to r + 3, for r a multiple of 8, at least one carries 1. `companion_group_indices`: the 2 entries of a row differ.
All inputs are finite; a program needn't handle non-finite values.
Results may differ from a plain program's by a relative error of at most 0.0003.
Values sent between devices are 32-bit elements; how exact they have to be, the bound alone decides.
No kernel may reach another device: no remote copies, remote signals or barrier semaphores. Data moves between devices by JAX's collectives and lax.ppermute only.
A program may use at most 64 MiB of HBM per device.

v0:
```python
import jax
import jax.numpy as jnp
from jax import lax
from jax.experimental import pallas as pl
from jax.experimental.pallas import tpu as pltpu
from jax.sharding import PartitionSpec as P

TIME_STEP = 0.05
THERMO_RELAX = 0.5
KINETIC_EPSILON = 1e-06
LOG2E = 1.4426950408889634
FAR = -1.0e5

F32 = jnp.float32
BF16 = jnp.bfloat16

LANES = 128
EDGE = 8
OWN = 64
ALL = OWN + EDGE
DUMMY = ALL
CHUNK = 4
CHUNKS = ALL // CHUNK
ROOM = ALL + CHUNK
LISTED = 2 * ROOM
GROUP = 8
FWD_PARTS = 1
BWD_PARTS = 2


def dot(a, b, ca, cb):
    return lax.dot_general(a, b, (((ca,), (cb,)), ((), ())), preferred_element_type=F32)


def split3(a):
    high = a.astype(BF16).astype(F32)
    rest = a - high
    mid = rest.astype(BF16).astype(F32)
    return high, mid, rest - mid


def factor_rows(left, right):
    lh, lm, ll = split3(left)
    rh, rm, rl = split3(right)
    return (
        jnp.concatenate([lh, lh, lm, lm, lh, ll], axis=1),
        jnp.concatenate([rh, rm, rh, rm, rl, rh], axis=1),
        rh,
        rm,
    )


def rows_of(shape):
    return lax.broadcasted_iota(jnp.int32, shape, 1)


def exponent_rows(x, row):
    coupling = jnp.log2(jnp.where(row == 6, x, 1.0))
    n = jnp.sum(
        jnp.where(row < 3, (-0.5 * LOG2E) * x * x, coupling), axis=1, keepdims=True
    )
    left = jnp.where(row < 3, LOG2E * x, jnp.where(row == 3, n, jnp.where(row == 4, 1.0, 0.0)))
    right = jnp.where(row < 3, x, jnp.where(row == 3, 1.0, jnp.where(row == 4, n, 0.0)))
    return left, right


def put_exponents(x, row, at, le, re, fx=None):
    left, right = exponent_rows(x, row)
    lrows, rrows, high, mid = factor_rows(left, right)
    le[at] = lrows
    re[at] = rrows.astype(BF16)
    if fx is not None:
        fx[at] = jnp.concatenate([high, mid], axis=1).astype(BF16)


def put_slopes(x, c, row, at, ld, rd, fx):
    x3 = pltpu.roll(x, 3, 1)
    c3 = pltpu.roll(c, 3, 1)
    s = jnp.sum(jnp.where(row < 3, x * c, 0.0), axis=1, keepdims=True)
    left = jnp.where(row < 3, c, jnp.where(row < 6, x3, jnp.where(row == 6, s, 1.0)))
    right = jnp.where(row < 3, -x, jnp.where(row < 6, -c3, jnp.where(row == 6, 1.0, s)))
    lrows, rrows, high, mid = factor_rows(left, right)
    ld[at] = lrows
    rd[at] = rrows.astype(BF16)
    fx[at] = jnp.concatenate([high, mid], axis=1).astype(BF16)


def put_dummy(le, re, fx, more=()):
    row = lax.broadcasted_iota(jnp.int32, (48, LANES), 0)
    le[DUMMY] = jnp.zeros((48, LANES), F32)
    re[DUMMY] = jnp.where((row == 4) | (row == 20), FAR, 0.0).astype(BF16)
    fx[DUMMY] = jnp.zeros((16, LANES), BF16)
    for ref, dtype in more:
        ref[DUMMY] = jnp.zeros((48, LANES), dtype)


def pair_sums(qs, base, le, re, fx, outs, weights, parts, slopes=None):
    def stage(chunk, bufs):
        for u in range(CHUNK):
            p = chunk * CHUNK + u
            q1 = qs[base + 2 * p]
            q2 = qs[base + 2 * p + 1]
            left = jnp.transpose(le[p]).astype(BF16)
            right = jnp.concatenate([re[q1], re[q2]], axis=1)
            w = jnp.exp2(dot(left, right, 1, 0))
            values = [w]
            if slopes is not None:
                ld, rd = slopes
                left = jnp.transpose(ld[p]).astype(BF16)
                right = jnp.concatenate([rd[q1], rd[q2]], axis=1)
                values.append(w * dot(left, right, 1, 0))
            for buf, value in zip(bufs, values):
                high = value.astype(BF16)
                buf[u, 0] = high
                if parts == 2:
                    buf[u, 1] = (value - high.astype(F32)).astype(BF16)

    def drain(chunk, bufs):
        found = []
        for u in range(CHUNK):
            p = chunk * CHUNK + u
            q1 = qs[base + 2 * p]
            q2 = qs[base + 2 * p + 1]
            fp = fx[p]
            fq = jnp.concatenate([fx[q1], fx[q2]], axis=1)
            for out, buf in zip(outs, bufs):
                to_p = 0.0
                to_q = 0.0
                for k in range(parts):
                    w = buf[u, k]
                    to_q = to_q + dot(fp, w, 1, 0)
                    to_p = to_p + dot(fq, w, 1, 1)
                found.append((out, p, q1, q2, to_p[:8] + to_p[8:], to_q[:8] + to_q[8:]))
        for out, p, q1, q2, to_p, to_q in found:
            out[p] += to_p
            out[q1] += to_q[:, :LANES]
            out[q2] += to_q[:, LANES:]

    even, odd = weights
    stage(0, even)

    def step(i, carry):
        drain(2 * i, even)
        stage(2 * i + 1, odd)
        drain(2 * i + 1, odd)
        stage(2 * i + 2, even)
        return carry

    lax.fori_loop(0, CHUNKS // 2, step, 0)


def row_total(block, r):
    row = lax.broadcasted_iota(jnp.int32, block.shape, 0)
    return jnp.sum(jnp.where(row == r, block, 0.0), keepdims=True)


def block_sum(a):
    return jnp.sum(a, axis=0)


def thermostat(total_k, target, atoms_all):
    state = 2.0 * total_k / (3 * atoms_all) + KINETIC_EPSILON
    return state, jnp.sqrt(1.0 + THERMO_RELAX * (target / state - 1.0))


def put_message(msg, state, sums, edge):
    msg[0:EDGE] = state[pl.ds(edge, EDGE)]
    row = lax.broadcasted_iota(jnp.int32, (8, LANES), 0)
    block = jnp.zeros((8, LANES), F32)
    for r, value in enumerate(sums):
        if value is not None:
            total = jnp.sum(value, axis=0, keepdims=True)
            block = block + jnp.where(row == r, total, 0.0)
    msg[EDGE] = block


def group_rows():
    return rows_of((GROUP, 8, LANES))


def over_groups(body, init=0):
    return lax.fori_loop(0, OWN // GROUP, lambda i, c: body(pl.ds(i * GROUP, GROUP), c), init)


def clear(*accs):
    def body(at, carry):
        for acc in accs:
            acc[at] = jnp.zeros((GROUP, 8, LANES), F32)
        return carry

    over_groups(body)
    for acc in accs:
        acc[pl.ds(OWN, EDGE)] = jnp.zeros((EDGE, 8, LANES), F32)
        acc[DUMMY] = jnp.zeros((8, LANES), F32)


def forward_kernel(n, steps, atoms_all):
    half_step = 0.5 * TIME_STEP
    last = n == steps
    base = n * LISTED
    zero = (8, LANES)

    def body(*refs):
        refs = list(refs)
        ints, temps, xu, got = refs[:4]
        del refs[:4]
        if n > 0:
            g, sent = refs[:2]
            del refs[:2]
        if last:
            adj, self_sum = refs[:2]
            del refs[:2]
        xu_out, g_out, xh_out, msg = refs[:4]
        del refs[:4]
        if n > 1:
            scal = refs.pop(0)
        le, re, fx, acc, tmp, w0, w1 = refs
        edge = ints[(steps + 1) * LISTED]
        if n > 0:
            factor = jnp.ones((1, 1), F32)
            if n > 1:
                both = sent[EDGE] + got[EDGE]
                target = temps[0] if n - 2 < steps // 2 else temps[1]
                present, factor = thermostat(row_total(both, 0), target, atoms_all)
                r8 = lax.broadcasted_iota(jnp.int32, zero, 0)
                scal[...] = jnp.where(
                    r8 == 0, jnp.broadcast_to(factor, zero), jnp.broadcast_to(present, zero)
                )
                if n - 1 == steps // 2:
                    factor = factor * temps[2]
            factor = factor.reshape(1, 1, 1)

        def prepare(at, carry):
            row = group_rows()
            state = xu[at]
            mid = pltpu.roll(state, 5, 1)
            if n > 0:
                mid = factor * mid + g[at]
                state = jnp.where(row < 3, state + TIME_STEP * mid, state)
            tmp[at] = mid
            xu_out[at] = state
            put_exponents(state, row, at, le, re, fx)
            return carry

        over_groups(prepare)
        row = rows_of((EDGE, 8, LANES))
        halo = got[0:EDGE]
        if n > 0:
            halo = jnp.where(row < 3, halo + (TIME_STEP * factor) * pltpu.roll(halo, 5, 1), halo)
        xh_out[...] = halo
        put_exponents(halo, row, pl.ds(OWN, EDGE), le, re, fx)
        put_dummy(le, re, fx)
        clear(acc)
        pair_sums(ints, base, le, re, fx, (acc,), ((w0,), (w1,)), FWD_PARTS)

        def finish(at, carry):
            row = group_rows()
            three = row < 3
            state = xu_out[at]
            high = state.astype(BF16).astype(F32)
            sums = acc[at]
            total = sums[:, 3:4, :]
            force = 0.25 * ((high + (state - high).astype(BF16).astype(F32)) * total - sums)
            inv_mass = state[:, 7:8, :]
            pull = half_step * inv_mass * force
            updated = tmp[at]
            if n > 0:
                updated = updated + pull
            g_out[at] = pull
            state = jnp.where((row >= 3) & (row < 6), pltpu.roll(updated, 3, 1), state)
            xu_out[at] = state
            found = [block_sum(jnp.where(three, 0.5 * updated * updated / inv_mass, 0.0))]
            if last:
                cot_v = pltpu.roll(adj[at], 5, 1)
                found.append(block_sum(jnp.where(row == 3, 0.125 * sums, 0.0)))
                found.append(block_sum(jnp.where(three, cot_v * updated, 0.0)))
                tmp[at] = jnp.where(three, half_step * inv_mass * cot_v, state)
            else:
                tmp[at] = jnp.where(three, state + TIME_STEP * pull, state)
            return tuple(c + f for c, f in zip(carry, found))

        partial = list(over_groups(finish, (jnp.zeros(zero, F32),) * (3 if last else 1)))
        if last:
            partial[1] = partial[1] - self_sum[...]
        put_message(msg, tmp, partial, edge)

    return body


def backward_kernel(n, steps, atoms_all):
    half_step = 0.5 * TIME_STEP
    first = n == steps
    swap_at = steps // 2
    base = n * LISTED
    zero = (8, LANES)

    def body(*refs):
        refs = list(refs)
        ints, temps, xu, xh, av, got = refs[:6]
        del refs[:6]
        if n > 0:
            sent = refs.pop(0)
        if 0 < n < steps:
            uh, scal = refs[:2]
            del refs[:2]
        if n > 1:
            before = refs.pop(0)
        if n == 0:
            final = refs.pop(0)
        av_out = refs.pop(0)
        if n > 0:
            msg = refs.pop(0)
        if first:
            fv_out = refs.pop(0)
        le, re, fx, ld, rd, acc_w, acc_v, tmp, w0, w1, v0, v1 = refs
        edge = ints[(steps + 1) * LISTED]
        if n > 0:
            both = sent[EDGE] + got[EDGE]
            target = temps[0] if n - 1 < swap_at else temps[1]
            if first:
                present, factor = thermostat(row_total(both, 0), target, atoms_all)
                energy = (row_total(both, 1) / atoms_all).reshape(1, 1, 1)
            else:
                factor = scal[0:1, 0:1]
                present = scal[1:2, 0:1]
            inner = row_total(both, 2)
            slope = (
                (-THERMO_RELAX)
                * target
                / (present * present)
                * (2.0 / (3 * atoms_all))
                / (2.0 * factor)
            )
            kappa = (inner * slope).reshape(1, 1, 1)
            factor = factor.reshape(1, 1, 1)
            if first:
                weight = factor
            elif n == swap_at:
                weight = factor + temps[3]
            else:
                weight = factor + 1.0

        def prepare(at, carry):
            row = group_rows()
            state = xu[at]
            inv_mass = state[:, 7:8, :]
            cot_v = pltpu.roll(av[at], 5, 1)
            own_c = half_step * inv_mass * cot_v
            if n > 0:
                updated = pltpu.roll(state, 5, 1)
                tmp[at] = factor * cot_v + kappa * updated / inv_mass
                own_c = weight * own_c + (half_step * kappa) * updated
                if first:
                    fv_out[at] = jnp.where(row < 3, state, factor * state)
            put_exponents(state, row, at, le, re)
            put_slopes(state, own_c, row, at, ld, rd, fx)
            return carry

        over_groups(prepare)
        row = rows_of((EDGE, 8, LANES))
        halo = xh[...]
        halo_c = got[0:EDGE]
        if n > 0:
            partner_u = halo_c if first else uh[0:EDGE]
            halo_c = weight * halo_c + (half_step * kappa) * pltpu.roll(partner_u, 5, 1)
        put_exponents(halo, row, pl.ds(OWN, EDGE), le, re)
        put_slopes(halo, halo_c, row, pl.ds(OWN, EDGE), ld, rd, fx)
        put_dummy(le, re, fx, ((ld, F32), (rd, BF16)))
        clear(acc_w, acc_v)
        pair_sums(
            ints,
            base,
            le,
            re,
            fx,
            (acc_w, acc_v),
            ((w0, v0), (w1, v1)),
            BWD_PARTS,
            slopes=(ld, rd),
        )

        def finish(at, carry):
            row = group_rows()
            three = row < 3
            own = fx[at].astype(F32)
            own = own[:, :8] + own[:, 8:]
            sums_w = acc_w[at]
            sums_v = acc_v[at]
            total_v = sums_v[:, 6:7, :]
            from_w = pltpu.roll(sums_w - own * sums_w[:, 6:7, :], 5, 1)
            gradient = 0.25 * (from_w - (sums_v - own * total_v))
            state = xu[at]
            inv_mass = state[:, 7:8, :]
            cot = av[at]
            cot = jnp.where(three, cot + gradient, cot)
            cot = jnp.where(row == 6, cot + 0.25 * total_v / state[:, 6:7, :], cot)
            if n == 0:
                av_out[at] = jnp.concatenate([final[at], cot], axis=1)
                return carry
            cot_mid = tmp[at] + TIME_STEP * cot
            if n - 1 == swap_at:
                cot_mid = cot_mid * temps[2]
            if first:
                cot = jnp.where(row == 7, energy, cot)
            cot = jnp.where((row >= 3) & (row < 6), pltpu.roll(cot_mid, 3, 1), cot)
            av_out[at] = cot
            tmp[at] = jnp.where(three, half_step * inv_mass * cot_mid, 0.0)
            if n > 1:
                held = pltpu.roll(before[at], 5, 1)
                carry = carry + block_sum(jnp.where(three, cot_mid * held, 0.0))
            return carry

        inner = over_groups(finish, jnp.zeros(zero, F32))
        if n > 0:
            put_message(msg, tmp, [None, None, inner if n > 1 else None], edge)

    return body


def shape(*dims):
    return pltpu.VMEM(dims, F32)


def vmem():
    return pl.BlockSpec(memory_space=pltpu.VMEM)


def smem():
    return pl.BlockSpec(memory_space=pltpu.SMEM)


def scratch_of(backward):
    blocks = ROOM
    parts = BWD_PARTS if backward else FWD_PARTS
    weight = pltpu.VMEM((CHUNK, parts, LANES, 2 * LANES), BF16)
    acc = pltpu.VMEM((blocks, 8, LANES), F32)
    left = pltpu.VMEM((blocks, 48, LANES), F32)
    right = pltpu.VMEM((blocks, 48, LANES), BF16)
    found = [left, right, pltpu.VMEM((blocks, 16, LANES), BF16)]
    if backward:
        found += [left, right, acc]
    found += [acc, pltpu.VMEM((OWN, 8, LANES), F32), weight, weight]
    if backward:
        found += [weight, weight]
    return found


def run_kernel(body, name, ints, temps, arrays, out_shapes, backward):
    arrays = [pltpu.with_memory_space_constraint(a, pltpu.VMEM) for a in arrays]
    return pl.pallas_call(
        body,
        in_specs=[smem(), smem()] + [vmem() for _ in arrays],
        out_specs=[vmem() for _ in out_shapes],
        out_shape=out_shapes,
        scratch_shapes=scratch_of(backward),
        name=name,
    )(ints, temps, *arrays)


def quarter_spot(i):
    return (0, 2, 1, 3)[i]


def local(
    starting_locations,
    starting_speeds,
    terminal_location_adjoint,
    terminal_speed_adjoint,
    interaction_strength,
    reciprocal_particle_weight,
    heat_levels,
    swap_indicator,
    companion_group_indices,
):
    count = lax.axis_size("atom")
    atoms_all = starting_locations.shape[2] * count
    steps = companion_group_indices.shape[0] - 1
    spot = lax.axis_index("atom")
    lane_of_four = spot % 4
    core = spot % 2
    replica = spot // 4

    partner = lax.ppermute(heat_levels, "rep", [(i, i ^ 1) for i in range(lax.axis_size("rep"))])
    later = jnp.where(swap_indicator == 1, partner, heat_levels)
    mine = jnp.arange(4) == replica
    t1 = jnp.sum(jnp.where(mine, heat_levels, 0.0))
    t2 = jnp.sum(jnp.where(mine, later, 0.0))
    temps = jnp.stack([t1, t2, jnp.sqrt(t2 / t1), jnp.sqrt(t1 / t2)])

    def blocks(a):
        return a.reshape(a.shape[0], a.shape[1], EDGE, LANES).transpose(0, 2, 1, 3)

    shared = jnp.stack([interaction_strength, reciprocal_particle_weight])
    shared = jnp.broadcast_to(shared[None], (4, *shared.shape))
    start = blocks(jnp.concatenate([starting_locations, starting_speeds, shared], axis=1))
    adjoint = blocks(
        jnp.concatenate(
            [terminal_location_adjoint, terminal_speed_adjoint, jnp.zeros_like(shared)], axis=1
        )
    )
    lists = companion_group_indices.astype(F32).reshape(1, 1, 1, -1)
    lists = jnp.pad(lists, ((0, 0), (0, 0), (0, 7), (0, LANES - lists.shape[3])))
    lists = jnp.broadcast_to(lists, (4, 1, 8, LANES))
    outgoing = jnp.concatenate([start, lists, adjoint], axis=1)
    quarter = []
    for s in range(4):
        sent = lax.dynamic_index_in_dim(outgoing, (lane_of_four + s) % 4, 0, False)
        quarter.append(
            lax.ppermute(
                sent,
                "atom",
                [(i, 4 * ((i % 4 + s) % 4) + quarter_spot(i // 4)) for i in range(count)],
            )
        )
    order = jnp.concatenate([q[None] for q in reversed(quarter)] * 2, axis=0)
    quarter = lax.dynamic_slice_in_dim(order, (3 - replica) % 4, 4, 0)
    swap = [(i, i ^ 2) for i in range(count)]
    bit = (spot // 2) % 2

    def both_quarters(a):
        other = lax.ppermute(a, "atom", swap)
        low = jnp.where(bit == 0, a, other)
        high = jnp.where(bit == 0, other, a)
        return jnp.concatenate([low, high], axis=0)

    early = both_quarters(quarter[:, : EDGE + 1])
    late = both_quarters(quarter[:, EDGE + 1 :])
    xu = early[:, :EDGE].reshape(OWN, 8, LANES)
    adj = late.reshape(OWN, 8, LANES)
    pair = [(i, i ^ 1) for i in range(count)]

    def exchange(a):
        return lax.ppermute(a, "atom", pair)

    beside = jnp.where(core == 0, early[-1], early[0])
    got = exchange(beside)
    edge = jnp.where(core == 0, OWN - EDGE, 0).astype(jnp.int32)

    def listed(a):
        return a[..., EDGE, 0, : 10 * EDGE].astype(jnp.int32)

    slots = listed(early).reshape(8, 5, EDGE, 2).transpose(1, 0, 2, 3)
    shard = 8 * core + jnp.arange(8, dtype=jnp.int32)
    block = (shard * EDGE - EDGE)[None, :, None, None] + slots
    block = block.reshape(5, OWN, 2)
    here = block - OWN * core
    halo_first = jnp.where(core == 0, OWN, OWN - EDGE)
    beyond = block - halo_first
    own_q = jnp.where(
        (here >= 0) & (here < OWN),
        here,
        jnp.where((beyond >= 0) & (beyond < EDGE), OWN + beyond, DUMMY),
    )
    halo_shard = jnp.where(core == 0, 8, 7)
    halo_q = listed(got).reshape(5, EDGE, 2) + (halo_shard * EDGE - EDGE) - OWN * core
    halo_q = jnp.where((halo_q >= 0) & (halo_q < OWN), halo_q, DUMMY)
    pairs = jnp.concatenate([own_q, halo_q], axis=1)
    pairs = jnp.pad(pairs, ((0, 0), (0, ROOM - ALL), (0, 0)), constant_values=DUMMY)
    ints = jnp.concatenate([pairs.reshape(-1), jnp.broadcast_to(edge, (8,))])
    selves = jnp.any(own_q[steps] == jnp.arange(OWN, dtype=jnp.int32)[:, None], axis=1)
    self_sum = jnp.sum(
        jnp.where(selves[:, None], 0.25 * xu[:, 6, :] * xu[:, 6, :], 0.0), axis=0, keepdims=True
    )
    self_sum = jnp.pad(self_sum, ((0, 7), (0, 0)))

    full = shape(OWN, 8, LANES)
    part = shape(EDGE, 8, LANES)
    message = shape(EDGE + 1, 8, LANES)
    scalars = shape(8, LANES)

    states, halos, received, sents, scal = [], [], [got], [None], {}
    g = None
    for n in range(steps + 1):
        arrays = [xu, received[n]]
        if n > 0:
            arrays += [g, sents[n]]
        if n == steps:
            arrays += [adj, self_sum]
        outs = [full, full, part, message]
        if n > 1:
            outs.append(scalars)
        found = run_kernel(
            forward_kernel(n, steps, atoms_all),
            f"force_{n}",
            ints,
            temps,
            arrays,
            outs,
            False,
        )
        xu, g, xh, msg = found[:4]
        if n > 1:
            scal[n - 1] = found[4]
        states.append(xu)
        halos.append(xh)
        sents.append(msg)
        received.append(exchange(msg))

    av = adj
    got, sent = received[steps + 1], sents[steps + 1]
    for n in reversed(range(steps + 1)):
        arrays = [states[n], halos[n], av, got]
        if n > 0:
            arrays.append(sent)
        if 0 < n < steps:
            arrays += [received[n + 1], scal[n]]
        if n > 1:
            arrays.append(states[n - 1])
        if n == 0:
            arrays.append(final)
        outs = [full, message] if n > 0 else [shape(OWN, 16, LANES)]
        if n == steps:
            outs.append(full)
        found = run_kernel(
            backward_kernel(n, steps, atoms_all), f"adjoint_{n}", ints, temps, arrays, outs, True
        )
        av = found[0]
        if n == steps:
            final = found[2]
        if n > 0:
            sent = found[1]
            got = exchange(sent)

    results = av.reshape(8, EDGE, 16, LANES)
    returned = []
    for s in range(4):
        kk = (replica - s) % 4
        piece = lax.dynamic_index_in_dim(results, 4 * bit + kk, 0, False)
        returned.append(
            lax.ppermute(
                piece,
                "atom",
                [(4 * ((i % 4 + s) % 4) + quarter_spot(i // 4), i) for i in range(count)],
            )
        )
    order = jnp.concatenate([r[None] for r in returned] * 2, axis=0)
    back = lax.dynamic_slice_in_dim(order, (4 - lane_of_four) % 4, 4, 0)

    def rows(first, size):
        a = back[:, :, first : first + size].transpose(0, 2, 1, 3)
        return a.reshape(4, size, EDGE * LANES)

    energies = back[:, 0, 15, 0]
    coupling = jnp.sum(back[:, :, 14], axis=0).reshape(-1)
    copies = jnp.broadcast_to(coupling, (lax.axis_size("rep"), *coupling.shape))
    everything = lax.all_to_all(copies, "rep", split_axis=0, concat_axis=0, tiled=True)
    grad_coupling = jnp.sum(everything, axis=0)
    return (rows(0, 3), rows(3, 3), energies, rows(8, 3), rows(11, 3), grad_coupling)


def solution(mesh):
    in_specs = (
        P("rep", None, "atom"),
        P("rep", None, "atom"),
        P("rep", None, "atom"),
        P("rep", None, "atom"),
        P("atom"),
        P("atom"),
        P("rep"),
        P("rep"),
        P(None, "atom", None),
    )
    out_specs = (
        P("rep", None, "atom"),
        P("rep", None, "atom"),
        P("rep"),
        P("rep", None, "atom"),
        P("rep", None, "atom"),
        P("atom"),
    )
    return jax.shard_map(local, mesh=mesh, in_specs=in_specs, out_specs=out_specs, check_vma=False)
```

profile of v0, /device:TPU:32, one launch (start us, length us, event | category | flops | bytes accessed | tf_op | source)
XLA Modules:
  0.0 186.7 jit_solution(14522824963442407231)
XLA Ops:
  3.7 6.0 %collective-permute-start = (f32[17,8,128]{2,1,0:T(8,128)S(1)}, f32[17,8,128]{2,1,0:T(8,128)S(1)}, u32[]{:S(2)}, u32[]{:S(2)}) collective-permute-start(f32[17,8,128]{2,1,0:T(8,128)S(1)} %get-tuple-element.83), channel_id=1, source_target_pairs={{0,12},{1,0},{2,4},{3,8},{4,14},{5,2},{6,6},{7,10},{8,13},{9,1},{1... | collective-permute-start | bytes 208904 | tf_op jit(solution)/shard_map/ppermute | solution.py:509
  9.8 3.4 %collective-permute-start.2 = (f32[17,8,128]{2,1,0:T(8,128)S(1)}, f32[17,8,128]{2,1,0:T(8,128)S(1)}, u32[]{:S(2)}, u32[]{:S(2)}) collective-permute-start(f32[17,8,128]{2,1,0:T(8,128)S(1)} %get-tuple-element.81), channel_id=1, source_target_pairs={{0,4},{1,8},{2,12},{3,0},{4,6},{5,10},{6,14},{7,2},{8,5},{9,9},{10... | collective-permute-start | bytes 208904 | tf_op jit(solution)/shard_map/ppermute | solution.py:509
  14.2 3.4 %collective-permute-done.6 = f32[4]{0:T(128)S(1)} collective-permute-done((f32[4]{0:T(128)S(1)}, f32[4]{0:T(128)S(1)}, u32[]{:S(2)}, u32[]{:S(2)}) %collective-permute-start.6) | collective-permute-done | bytes 48 | tf_op jit(solution)/shard_map/ppermute | solution.py:483
  21.2 3.8 %collective-permute-start.4 = (f32[4,9,8,128]{3,2,1,0:T(8,128)S(1)}, f32[4,9,8,128]{3,2,1,0:T(8,128)S(1)}, u32[]{:S(2)}, u32[]{:S(2)}) collective-permute-start(f32[4,9,8,128]{3,2,1,0:T(8,128)S(1)} %constant_dynamic-slice_fusion.1), channel_id=1, source_target_pairs={{0,2},{1,3},{2,0},{3,1},{4,6},{5,7},{6,4},{7,5},{8,10},{9,11},{10,... | collective-permute-start | bytes 442376 | tf_op jit(solution)/shard_map/ppermute | solution.py:521
  25.0 1.9 %pad_maximum_fusion.5.refs_1_ = f32[4]{0:T(128)} fusion(f32[1]{0:T(128)} %bitcast.20, f32[1]{0:T(128)} %bitcast.19, f32[1]{0:T(128)} %bitcast.18, f32[1]{0:T(128)} %bitcast.17), kind=kLoop, calls=%fused_computation.69 | loop fusion | flops 12 | bytes 32 | tf_op jit(solution)/shard_map/stack | solution.py:488
  27.0 2.7 %collective-permute-done.4 = f32[4,9,8,128]{3,2,1,0:T(8,128)S(1)} collective-permute-done((f32[4,9,8,128]{3,2,1,0:T(8,128)S(1)}, f32[4,9,8,128]{3,2,1,0:T(8,128)S(1)}, u32[]{:S(2)}, u32[]{:S(2)}) %collective-permute-start.4) | collective-permute-done | bytes 147488 | tf_op jit(solution)/shard_map/ppermute | solution.py:521
  30.4 1.2 collective-permute-done.5.refs_3_
  32.8 6.9 %force_0.1 = (f32[64,8,128]{2,1,0:T(8,128)S(1)}, f32[64,8,128]{2,1,0:T(8,128)S(1)}, f32[8,8,128]{2,1,0:T(8,128)S(1)}, f32[9,8,128]{2,1,0:T(8,128)S(1)}) custom-call(s32[768]{0:T(1024)} %concatenate.33.refs_0_, f32[4]{0:T(128)} %pad_maximum_fusion.5.refs_1_, f32[64,8,128]{2,1,0:T(8,128)S(1)} %bitcast.107, f32[9,8,128]{2,1,0:T(8,128)S(1)} %collective-permute-done.5.refs_3_), custom_call_target="tpu_custom_call" | custom-call | tf_op jit(solution)/shard_map/force_0/pallas_call | solution.py:450
  41.0 6.9 %force_1.1 = (f32[64,8,128]{2,1,0:T(8,128)S(1)}, f32[64,8,128]{2,1,0:T(8,128)S(1)}, f32[8,8,128]{2,1,0:T(8,128)S(1)}, f32[9,8,128]{2,1,0:T(8,128)S(1)}) custom-call(s32[768]{0:T(1024)} %concatenate.33.refs_0_, f32[4]{0:T(128)} %pad_maximum_fusion.5.refs_1_, f32[64,8,128]{2,1,0:T(8,128)S(1)} %get-tuple-element.37.refs_2_, ...), custom_call_target="tpu_custom_call" | custom-call | tf_op jit(solution)/shard_map/force_1/pallas_call | solution.py:450
  49.2 7.1 %force_2.1 = (f32[64,8,128]{2,1,0:T(8,128)S(1)}, f32[64,8,128]{2,1,0:T(8,128)S(1)}, f32[8,8,128]{2,1,0:T(8,128)S(1)}, f32[9,8,128]{2,1,0:T(8,128)S(1)}, f32[8,128]{1,0:T(8,128)S(1)}) custom-call(s32[768]{0:T(1024)} %concatenate.33.refs_0_, f32[4]{0:T(128)} %pad_maximum_fusion.5.refs_1_, f32[64,8,128]{2,1,0:T(8,128)S(1)} %get-tuple-element.41.refs_2_.refs_9_, ...), custom_call_target="tpu_custom_call" | custom-call | tf_op jit(solution)/shard_map/force_2/pallas_call | solution.py:450
  57.6 7.1 %force_3.1 = (f32[64,8,128]{2,1,0:T(8,128)S(1)}, f32[64,8,128]{2,1,0:T(8,128)S(1)}, f32[8,8,128]{2,1,0:T(8,128)S(1)}, f32[9,8,128]{2,1,0:T(8,128)S(1)}, f32[8,128]{1,0:T(8,128)S(1)}) custom-call(s32[768]{0:T(1024)} %concatenate.33.refs_0_, f32[4]{0:T(128)} %pad_maximum_fusion.5.refs_1_, f32[64,8,128]{2,1,0:T(8,128)S(1)} %get-tuple-element.45.refs_2_.refs_9_, ...), custom_call_target="tpu_custom_call" | custom-call | tf_op jit(solution)/shard_map/force_3/pallas_call | solution.py:450
  66.0 7.8 %force_4.1 = (f32[64,8,128]{2,1,0:T(8,128)S(1)}, f32[64,8,128]{2,1,0:T(8,128)}, f32[8,8,128]{2,1,0:T(8,128)S(1)}, f32[9,8,128]{2,1,0:T(8,128)S(1)}, f32[8,128]{1,0:T(8,128)S(1)}) custom-call(s32[768]{0:T(1024)} %concatenate.33.refs_0_, f32[4]{0:T(128)} %pad_maximum_fusion.5.refs_1_, f32[64,8,128]{2,1,0:T(8,128)S(1)} %get-tuple-element.49.refs_2_.refs_7_, ...), custom_call_target="tpu_custom_call" | custom-call | tf_op jit(solution)/shard_map/force_4/pallas_call | solution.py:450
  75.0 13.7 %adjoint_4.1 = (f32[64,8,128]{2,1,0:T(8,128)S(1)}, f32[9,8,128]{2,1,0:T(8,128)S(1)}, f32[64,8,128]{2,1,0:T(8,128)S(1)}) custom-call(s32[768]{0:T(1024)} %concatenate.33.refs_0_, f32[4]{0:T(128)} %pad_maximum_fusion.5.refs_1_, f32[64,8,128]{2,1,0:T(8,128)S(1)} %get-tuple-element.53.refs_2_, f32[8,8,128]{2,1,0:T(8,128)S(1)} %get-tuple-element.54.refs_3_, ...), custom_call_target="tpu_custom_call" | custom-call | tf_op jit(solution)/shard_map/adjoint_4/pallas_call | solution.py:450
  90.0 13.8 %adjoint_3.1 = (f32[64,8,128]{2,1,0:T(8,128)S(1)}, f32[9,8,128]{2,1,0:T(8,128)S(1)}) custom-call(s32[768]{0:T(1024)} %concatenate.33.refs_0_, f32[4]{0:T(128)} %pad_maximum_fusion.5.refs_1_, f32[64,8,128]{2,1,0:T(8,128)S(1)} %get-tuple-element.49.refs_2_.refs_7_, f32[8,8,128]{2,1,0:T(8,128)S(1)} %get-tuple-element.50.refs_3_, ...), custom_call_target="tpu_custom_call" | custom-call | tf_op jit(solution)/shard_map/adjoint_3/pallas_call | solution.py:450
  105.1 13.8 %adjoint_2.1 = (f32[64,8,128]{2,1,0:T(8,128)S(1)}, f32[9,8,128]{2,1,0:T(8,128)S(1)}) custom-call(s32[768]{0:T(1024)} %concatenate.33.refs_0_, f32[4]{0:T(128)} %pad_maximum_fusion.5.refs_1_, f32[64,8,128]{2,1,0:T(8,128)S(1)} %get-tuple-element.45.refs_2_.refs_9_, f32[8,8,128]{2,1,0:T(8,128)S(1)} %get-tuple-element.46.refs_3_, ...), custom_call_target="tpu_custom_call" | custom-call | tf_op jit(solution)/shard_map/adjoint_2/pallas_call | solution.py:450
  120.3 13.8 %adjoint_1.1 = (f32[64,8,128]{2,1,0:T(8,128)S(1)}, f32[9,8,128]{2,1,0:T(8,128)S(1)}) custom-call(s32[768]{0:T(1024)} %concatenate.33.refs_0_, f32[4]{0:T(128)} %pad_maximum_fusion.5.refs_1_, f32[64,8,128]{2,1,0:T(8,128)S(1)} %get-tuple-element.41.refs_2_.refs_9_, f32[8,8,128]{2,1,0:T(8,128)S(1)} %get-tuple-element.42.refs_3_, ...), custom_call_target="tpu_custom_call" | custom-call | tf_op jit(solution)/shard_map/adjoint_1/pallas_call | solution.py:450
  135.4 13.3 %adjoint_0.1 = f32[64,16,128]{2,1,0:T(8,128)S(1)} custom-call(s32[768]{0:T(1024)} %concatenate.33.refs_0_, f32[4]{0:T(128)} %pad_maximum_fusion.5.refs_1_, f32[64,8,128]{2,1,0:T(8,128)S(1)} %get-tuple-element.37.refs_2_, f32[8,8,128]{2,1,0:T(8,128)S(1)} %get-tuple-element.38.refs_3_, f32[64,8,128]{2,1,0:T(8,128)S(1)} %get-tuple-element.65.refs_4_, ...), custom_call_target="tpu_custom_call" | custom-call | tf_op jit(solution)/shard_map/adjoint_0/pallas_call | solution.py:450
  149.5 6.1 %collective-permute-start.18 = (f32[8,16,128]{2,1,0:T(8,128)S(1)}, f32[8,16,128]{2,1,0:T(8,128)S(1)}, u32[]{:S(2)}, u32[]{:S(2)}) collective-permute-start(f32[8,16,128]{2,1,0:T(8,128)S(1)} %get-tuple-element.76), channel_id=1, source_target_pairs={{4,0},{8,1},{12,2},{0,3},{6,4},{10,5},{14,6},{2,7},{5,8},{9,9},{13... | collective-permute-start | bytes 196616 | tf_op jit(solution)/shard_map/ppermute | solution.py:630
  155.6 1.3 collective-permute-start.19
  156.9 1.9 %collective-permute-start.20 = (f32[8,16,128]{2,1,0:T(8,128)S(1)}, f32[8,16,128]{2,1,0:T(8,128)S(1)}, u32[]{:S(2)}, u32[]{:S(2)}) collective-permute-start(f32[8,16,128]{2,1,0:T(8,128)S(1)} %get-tuple-element.74), channel_id=1, source_target_pairs={{12,0},{0,1},{4,2},{8,3},{14,4},{2,5},{6,6},{10,7},{13,8},{1,9},{5... | collective-permute-start | bytes 196616 | tf_op jit(solution)/shard_map/ppermute | solution.py:630
  158.9 1.1 collective-permute-done.19
  159.9 5.5 %collective-permute-done.20 = f32[8,16,128]{2,1,0:T(8,128)S(1)} collective-permute-done((f32[8,16,128]{2,1,0:T(8,128)S(1)}, f32[8,16,128]{2,1,0:T(8,128)S(1)}, u32[]{:S(2)}, u32[]{:S(2)}) %collective-permute-start.20) | collective-permute-done | bytes 65568 | tf_op jit(solution)/shard_map/ppermute | solution.py:630
  166.2 10.8 %all-to-all-start = ((f32[16,1,1024]{2,1,0:T(1,128)}), f32[16,1,1024]{2,1,0:T(1,128)S(1)}, u32[]{:S(2)}, u32[]{:S(2)}) async-start(f32[16,1,1024]{2,1,0:T(1,128)} %broadcast_in_dim.96), calls=%async_computation | async-start | bytes 131072 | tf_op jit(solution)/shard_map/all_to_all | solution.py:646
  180.2 5.8 %all-to-all-done = f32[16,1,1024]{2,1,0:T(1,128)S(1)} async-done(((f32[16,1,1024]{2,1,0:T(1,128)}), f32[16,1,1024]{2,1,0:T(1,128)S(1)}, u32[]{:S(2)}, u32[]{:S(2)}) %all-to-all-start) | async-done | bytes 65568 | tf_op jit(solution)/shard_map/all_to_all | solution.py:646
  (125 shorter events, 23.4 us)
Async XLA Ops:
  3.7 17.3 %collective-permute-start = (f32[17,8,128]{2,1,0:T(8,128)S(1)}, f32[17,8,128]{2,1,0:T(8,128)S(1)}, u32[]{:S(2)}, u32[]{:S(2)}) collective-permute-start(f32[17,8,128]{2,1,0:T(8,128)S(1)} %get-tuple-element.83), channel_id=1, source_target_pairs={{0,12},{1,0},{2,4},{3,8},{4,14},{5,2},{6,6},{7,10},{8,13},{9,1},{1... | collective-permute-start | bytes 208904 | tf_op jit(solution)/shard_map/ppermute | solution.py:509
  9.7 11.3 %collective-permute-start.1 = (f32[17,8,128]{2,1,0:T(8,128)S(1)}, f32[17,8,128]{2,1,0:T(8,128)S(1)}, u32[]{:S(2)}, u32[]{:S(2)}) collective-permute-start(f32[17,8,128]{2,1,0:T(8,128)S(1)} %get-tuple-element.82), channel_id=1, source_target_pairs={{0,8},{1,12},{2,0},{3,4},{4,10},{5,14},{6,2},{7,6},{8,9},{9,13},{1... | collective-permute-start | bytes 208904 | tf_op jit(solution)/shard_map/ppermute | solution.py:509
  9.8 4.1 %copy-start.7 = (f32[4]{0:T(128)S(1)}, f32[4]{0:T(128)}, u32[]{:S(2)}) copy-start(f32[4]{0:T(128)} %param.15) | copy-start | bytes 52
  9.8 11.2 %collective-permute-start.2 = (f32[17,8,128]{2,1,0:T(8,128)S(1)}, f32[17,8,128]{2,1,0:T(8,128)S(1)}, u32[]{:S(2)}, u32[]{:S(2)}) collective-permute-start(f32[17,8,128]{2,1,0:T(8,128)S(1)} %get-tuple-element.81), channel_id=1, source_target_pairs={{0,4},{1,8},{2,12},{3,0},{4,6},{5,10},{6,14},{7,2},{8,5},{9,9},{10... | collective-permute-start | bytes 208904 | tf_op jit(solution)/shard_map/ppermute | solution.py:509
  13.3 7.8 %collective-permute-start.3 = (f32[17,8,128]{2,1,0:T(8,128)S(1)}, f32[17,8,128]{2,1,0:T(8,128)S(1)}, u32[]{:S(2)}, u32[]{:S(2)}) collective-permute-start(f32[17,8,128]{2,1,0:T(8,128)S(1)} %get-tuple-element.80), channel_id=1, source_target_pairs={{0,0},{1,4},{2,8},{3,12},{4,2},{5,6},{6,10},{7,14},{8,1},{9,5},{10... | collective-permute-start | bytes 208904 | tf_op jit(solution)/shard_map/ppermute | solution.py:509
  14.0 3.7 %collective-permute-start.6 = (f32[4]{0:T(128)S(1)}, f32[4]{0:T(128)S(1)}, u32[]{:S(2)}, u32[]{:S(2)}) collective-permute-start(f32[4]{0:T(128)S(1)} %copy-done.7), channel_id=1, source_target_pairs={{0,16},{16,0},{32,48},{48,32},{64,80},{80,64},{96,112},{112,96},{1... | collective-permute-start | bytes 56 | tf_op jit(solution)/shard_map/ppermute | solution.py:483
  14.2 3.5 %copy-start.8 = (s32[4]{0:T(128)S(1)}, s32[4]{0:T(128)}, u32[]{:S(2)}) copy-start(s32[4]{0:T(128)} %param.16) | copy-start | bytes 52
  21.2 8.5 %collective-permute-start.4 = (f32[4,9,8,128]{3,2,1,0:T(8,128)S(1)}, f32[4,9,8,128]{3,2,1,0:T(8,128)S(1)}, u32[]{:S(2)}, u32[]{:S(2)}) collective-permute-start(f32[4,9,8,128]{3,2,1,0:T(8,128)S(1)} %constant_dynamic-slice_fusion.1), channel_id=1, source_target_pairs={{0,2},{1,3},{2,0},{3,1},{4,6},{5,7},{6,4},{7,5},{8,10},{9,11},{10,... | collective-permute-start | bytes 442376 | tf_op jit(solution)/shard_map/ppermute | solution.py:521
  26.9 13.0 %collective-permute-start.11 = (f32[4,8,8,128]{3,2,1,0:T(8,128)S(1)}, f32[4,8,8,128]{3,2,1,0:T(8,128)S(1)}, u32[]{:S(2)}, u32[]{:S(2)}) collective-permute-start(f32[4,8,8,128]{3,2,1,0:T(8,128)S(1)} %constant_dynamic-slice_fusion.2), channel_id=1, source_target_pairs={{0,2},{1,3},{2,0},{3,1},{4,6},{5,7},{6,4},{7,5},{8,10},{9,11},{10,... | collective-permute-start | bytes 393224 | tf_op jit(solution)/shard_map/ppermute | solution.py:521
  30.3 1.3 collective-permute-start.5
  39.7 1.3 collective-permute-start.7
  47.9 1.3 collective-permute-start.8
  56.3 1.3 collective-permute-start.9
  64.7 1.3 collective-permute-start.10
  73.8 1.2 collective-permute-start.12
  88.7 1.3 collective-permute-start.13
  103.8 1.3 collective-permute-start.14
  119.0 1.3 collective-permute-start.15
  134.1 1.3 collective-permute-start.16
  148.8 10.0 %collective-permute-start.17 = (f32[8,16,128]{2,1,0:T(8,128)S(1)}, f32[8,16,128]{2,1,0:T(8,128)S(1)}, u32[]{:S(2)}, u32[]{:S(2)}) collective-permute-start(f32[8,16,128]{2,1,0:T(8,128)S(1)} %get-tuple-element.77), channel_id=1, source_target_pairs={{0,0},{4,1},{8,2},{12,3},{2,4},{6,5},{10,6},{14,7},{1,8},{5,9},{9,... | collective-permute-start | bytes 196616 | tf_op jit(solution)/shard_map/ppermute | solution.py:630
  149.5 9.4 %collective-permute-start.18 = (f32[8,16,128]{2,1,0:T(8,128)S(1)}, f32[8,16,128]{2,1,0:T(8,128)S(1)}, u32[]{:S(2)}, u32[]{:S(2)}) collective-permute-start(f32[8,16,128]{2,1,0:T(8,128)S(1)} %get-tuple-element.76), channel_id=1, source_target_pairs={{4,0},{8,1},{12,2},{0,3},{6,4},{10,5},{14,6},{2,7},{5,8},{9,9},{13... | collective-permute-start | bytes 196616 | tf_op jit(solution)/shard_map/ppermute | solution.py:630
  155.6 4.3 %collective-permute-start.19 = (f32[8,16,128]{2,1,0:T(8,128)S(1)}, f32[8,16,128]{2,1,0:T(8,128)S(1)}, u32[]{:S(2)}, u32[]{:S(2)}) collective-permute-start(f32[8,16,128]{2,1,0:T(8,128)S(1)} %get-tuple-element.75), channel_id=1, source_target_pairs={{8,0},{12,1},{0,2},{4,3},{10,4},{14,5},{2,6},{6,7},{9,8},{13,9},{1... | collective-permute-start | bytes 196616 | tf_op jit(solution)/shard_map/ppermute | solution.py:630
  156.9 8.6 %collective-permute-start.20 = (f32[8,16,128]{2,1,0:T(8,128)S(1)}, f32[8,16,128]{2,1,0:T(8,128)S(1)}, u32[]{:S(2)}, u32[]{:S(2)}) collective-permute-start(f32[8,16,128]{2,1,0:T(8,128)S(1)} %get-tuple-element.74), channel_id=1, source_target_pairs={{12,0},{0,1},{4,2},{8,3},{14,4},{2,5},{6,6},{10,7},{13,8},{1,9},{5... | collective-permute-start | bytes 196616 | tf_op jit(solution)/shard_map/ppermute | solution.py:630
  166.2 19.9 %all-to-all-start = ((f32[16,1,1024]{2,1,0:T(1,128)}), f32[16,1,1024]{2,1,0:T(1,128)S(1)}, u32[]{:S(2)}, u32[]{:S(2)}) async-start(f32[16,1,1024]{2,1,0:T(1,128)} %broadcast_in_dim.96), calls=%async_computation | async-start | bytes 131072 | tf_op jit(solution)/shard_map/all_to_all | solution.py:646
  (7 other events, 5.3 us)
where the time goes:
time: 188 us; the launch traced here: 187 us
  Pallas kernels  104 us (55%)
  starting transfers between devices  37.3 us (20%)
  waiting for transfers between devices  29 us (15%)
  local copies, waits for them, and re-layouts  8.3 us (4%)
  between operations  4.11 us (2%)
  other arithmetic  3.71 us (2%)
    pallas_call x10, Pallas kernels, run_kernel(): pl.pallas_call(body, in_specs=[smem(), smem()] + [vmem() for _ in arrays]...  104 us
    all_to_all x1, starting transfers between devices, local(): lax.all_to_all(copies, 'rep', split_axis=0, concat_axis=0, tiled=True)  10.8 us
    ppermute x10, waiting for transfers between devices, exchange(): return lax.ppermute(a, 'atom', pair)  10.4 us
    ppermute x4, starting transfers between devices, local(): lax.ppermute(sent, 'atom', [(i, 4 * ((i % 4 + s) % 4) + quarter_spot(i //...  10.2 us
    ppermute x4, starting transfers between devices, local(): lax.ppermute(piece, 'atom', [(4 * ((i % 4 + s) % 4) + quarter_spot(i // 4...  9.99 us
    ppermute x4, waiting for transfers between devices, local(): lax.ppermute(piece, 'atom', [(4 * ((i % 4 + s) % 4) + quarter_spot(i // 4...  6.58 us
    all_to_all x1, waiting for transfers between devices, local(): lax.all_to_all(copies, 'rep', split_axis=0, concat_axis=0, tiled=True)  5.85 us
    ppermute x2, starting transfers between devices, both_quarters(): other = lax.ppermute(a, 'atom', swap)  3.94 us
  transfers between devices with their start and end apart: 22, of which 15 were waited for; matrix products, arithmetic and copies ran while one was open for 4% of the time, Pallas kernels for 4%

commit v1 on v0

--- a/solution.py
+++ b/solution.py
@@ -19,9 +19,9 @@
 OWN = 64
 ALL = OWN + EDGE
 DUMMY = ALL
-CHUNK = 4
-CHUNKS = ALL // CHUNK
-ROOM = ALL + CHUNK
+FWD_CHUNK = 9
+BWD_CHUNK = 4
+ROOM = ALL + max(FWD_CHUNK, BWD_CHUNK)
 LISTED = 2 * ROOM
 GROUP = 8
 FWD_PARTS = 1
@@ -94,59 +94,67 @@
         ref[DUMMY] = jnp.zeros((48, LANES), dtype)
 
 
-def pair_sums(qs, base, le, re, fx, outs, weights, parts, slopes=None):
-    def stage(chunk, bufs):
-        for u in range(CHUNK):
-            p = chunk * CHUNK + u
-            q1 = qs[base + 2 * p]
-            q2 = qs[base + 2 * p + 1]
-            left = jnp.transpose(le[p]).astype(BF16)
-            right = jnp.concatenate([re[q1], re[q2]], axis=1)
-            w = jnp.exp2(dot(left, right, 1, 0))
-            values = [w]
-            if slopes is not None:
-                ld, rd = slopes
-                left = jnp.transpose(ld[p]).astype(BF16)
-                right = jnp.concatenate([rd[q1], rd[q2]], axis=1)
-                values.append(w * dot(left, right, 1, 0))
-            for buf, value in zip(bufs, values):
-                high = value.astype(BF16)
-                buf[u, 0] = high
-                if parts == 2:
-                    buf[u, 1] = (value - high.astype(F32)).astype(BF16)
-
-    def drain(chunk, bufs):
+def pair_sums(qs, base, le, re, fx, outs, weights, parts, chunk, slopes=None):
+    def stage_one(index, u, bufs):
+        p = index * chunk + u
+        q1 = qs[base + 2 * p]
+        q2 = qs[base + 2 * p + 1]
+        left = jnp.transpose(le[p]).astype(BF16)
+        right = jnp.concatenate([re[q1], re[q2]], axis=1)
+        w = jnp.exp2(dot(left, right, 1, 0))
+        values = [w]
+        if slopes is not None:
+            ld, rd = slopes
+            left = jnp.transpose(ld[p]).astype(BF16)
+            right = jnp.concatenate([rd[q1], rd[q2]], axis=1)
+            values.append(w * dot(left, right, 1, 0))
+        for buf, value in zip(bufs, values):
+            high = value.astype(BF16)
+            buf[u, 0] = high
+            if parts == 2:
+                buf[u, 1] = (value - high.astype(F32)).astype(BF16)
+
+    def drain_one(index, u, bufs):
         found = []
-        for u in range(CHUNK):
-            p = chunk * CHUNK + u
-            q1 = qs[base + 2 * p]
-            q2 = qs[base + 2 * p + 1]
-            fp = fx[p]
-            fq = jnp.concatenate([fx[q1], fx[q2]], axis=1)
-            for out, buf in zip(outs, bufs):
-                to_p = 0.0
-                to_q = 0.0
-                for k in range(parts):
-                    w = buf[u, k]
-                    to_q = to_q + dot(fp, w, 1, 0)
-                    to_p = to_p + dot(fq, w, 1, 1)
-                found.append((out, p, q1, q2, to_p[:8] + to_p[8:], to_q[:8] + to_q[8:]))
+        p = index * chunk + u
+        q1 = qs[base + 2 * p]
+        q2 = qs[base + 2 * p + 1]
+        fp = fx[p]
+        fq = jnp.concatenate([fx[q1], fx[q2]], axis=1)
+        for out, buf in zip(outs, bufs):
+            to_p = 0.0
+            to_q = 0.0
+            for k in range(parts):
+                w = buf[u, k]
+                to_q = to_q + dot(fp, w, 1, 0)
+                to_p = to_p + dot(fq, w, 1, 1)
+            found.append((out, p, q1, q2, to_p[:8] + to_p[8:], to_q[:8] + to_q[8:]))
+        return found
+
+    def add(found):
         for out, p, q1, q2, to_p, to_q in found:
             out[p] += to_p
             out[q1] += to_q[:, :LANES]
             out[q2] += to_q[:, LANES:]
 
     even, odd = weights
-    stage(0, even)
+
+    def both(full_chunk, full, next_chunk, empty):
+        waiting = []
+        for u in range(chunk):
+            stage_one(next_chunk, u, empty)
+            waiting += drain_one(full_chunk, u, full)
+        add(waiting)
+
+    for u in range(chunk):
+        stage_one(0, u, even)
 
     def step(i, carry):
-        drain(2 * i, even)
-        stage(2 * i + 1, odd)
-        drain(2 * i + 1, odd)
-        stage(2 * i + 2, even)
+        both(2 * i, even, 2 * i + 1, odd)
+        both(2 * i + 1, odd, 2 * i + 2, even)
         return carry
 
-    lax.fori_loop(0, CHUNKS // 2, step, 0)
+    lax.fori_loop(0, ALL // (2 * chunk), step, 0)
 
 
 def row_total(block, r):
@@ -251,7 +259,7 @@
         put_exponents(halo, row, pl.ds(OWN, EDGE), le, re, fx)
         put_dummy(le, re, fx)
         clear(acc)
-        pair_sums(ints, base, le, re, fx, (acc,), ((w0,), (w1,)), FWD_PARTS)
+        pair_sums(ints, base, le, re, fx, (acc,), ((w0,), (w1,)), FWD_PARTS, FWD_CHUNK)
 
         def finish(at, carry):
             row = group_rows()
@@ -376,6 +384,7 @@
             (acc_w, acc_v),
             ((w0, v0), (w1, v1)),
             BWD_PARTS,
+            BWD_CHUNK,
             slopes=(ld, rd),
         )
 
@@ -432,7 +441,8 @@
 def scratch_of(backward):
     blocks = ROOM
     parts = BWD_PARTS if backward else FWD_PARTS
-    weight = pltpu.VMEM((CHUNK, parts, LANES, 2 * LANES), BF16)
+    chunk = BWD_CHUNK if backward else FWD_CHUNK
+    weight = pltpu.VMEM((chunk, parts, LANES, 2 * LANES), BF16)
     acc = pltpu.VMEM((blocks, 8, LANES), F32)
     left = pltpu.VMEM((blocks, 48, LANES), F32)
     right = pltpu.VMEM((blocks, 48, LANES), BF16)
@@ -524,9 +534,7 @@
         return jnp.concatenate([low, high], axis=0)
 
     early = both_quarters(quarter[:, : EDGE + 1])
-    late = both_quarters(quarter[:, EDGE + 1 :])
     xu = early[:, :EDGE].reshape(OWN, 8, LANES)
-    adj = late.reshape(OWN, 8, LANES)
     pair = [(i, i ^ 1) for i in range(count)]
 
     def exchange(a):
@@ -595,6 +603,9 @@
         halos.append(xh)
         sents.append(msg)
         received.append(exchange(msg))
+        if n == 0:
+            late, _ = lax.optimization_barrier((quarter[:, EDGE + 1 :], received[1]))
+            adj = both_quarters(late).reshape(OWN, 8, LANES)
 
     av = adj
     got, sent = received[steps + 1], sents[steps + 1]

time: 188 us -> 175 us (0.931)
  Pallas kernels: 104 us -> 94.7 us
  waiting for transfers between devices: 29 us -> 22.3 us
  starting transfers between devices: 37.3 us -> 41.1 us
    pallas_call x10, Pallas kernels: 104 us -> 94.7 us  [run_kernel(): pl.pallas_call(body, in_specs=[smem(), smem()] + [vmem() for _ in arrays]...]
    ppermute x1, waiting for transfers between devices: 3.45 us -> 0.01 us  [local(): lax.ppermute(heat_levels, 'rep', [(i, i ^ 1) for i in range(lax.axis_size...]
    ppermute x2, waiting for transfers between devices: 2.71 us -> 0.01 us  [both_quarters(): other = lax.ppermute(a, 'atom', swap)]
    ppermute x2, starting transfers between devices: 3.94 us -> 6.28 us  [both_quarters(): other = lax.ppermute(a, 'atom', swap)]
  transfers between devices with their start and end apart: 22 -> 22, of which waited for: 15 -> 13; matrix products, arithmetic and copies ran while one was open for 4% -> 3% of each run, Pallas kernels for 4% -> 10%
where the time goes in v1:
time: 175 us; the launch traced here: 174 us
  Pallas kernels  94.7 us (54%)
  starting transfers between devices  41.1 us (23%)
  waiting for transfers between devices  22.3 us (13%)
  local copies, waits for them, and re-layouts  8.3 us (5%)
  between operations  4.1 us (2%)
  other arithmetic  3.71 us (2%)
    pallas_call x10, Pallas kernels, run_kernel(): pl.pallas_call(body, in_specs=[smem(), smem()] + [vmem() for _ in arrays]...  94.7 us
    ppermute x4, starting transfers between devices, local(): lax.ppermute(piece, 'atom', [(4 * ((i % 4 + s) % 4) + quarter_spot(i // 4...  11.4 us
    all_to_all x1, starting transfers between devices, local(): lax.all_to_all(copies, 'rep', split_axis=0, concat_axis=0, tiled=True)  10.8 us
    ppermute x10, waiting for transfers between devices, exchange(): return lax.ppermute(a, 'atom', pair)  10.5 us
    ppermute x4, starting transfers between devices, local(): lax.ppermute(sent, 'atom', [(i, 4 * ((i % 4 + s) % 4) + quarter_spot(i //...  10.2 us
    ppermute x2, starting transfers between devices, both_quarters(): other = lax.ppermute(a, 'atom', swap)  6.28 us
    all_to_all x1, waiting for transfers between devices, local(): lax.all_to_all(copies, 'rep', split_axis=0, concat_axis=0, tiled=True)  5.85 us
    ppermute x4, waiting for transfers between devices, local(): lax.ppermute(piece, 'atom', [(4 * ((i % 4 + s) % 4) + quarter_spot(i // 4...  4.71 us
  transfers between devices with their start and end apart: 22, of which 13 were waited for; matrix products, arithmetic and copies ran while one was open for 3% of the time, Pallas kernels for 10%

profile of v1, /device:TPU:32, one launch (start us, length us, event | category | flops | bytes accessed | tf_op | source)
XLA Modules:
  0.0 174.3 jit_solution(18354697951452666635)
XLA Ops:
  3.7 6.0 %collective-permute-start = (f32[17,8,128]{2,1,0:T(8,128)S(1)}, f32[17,8,128]{2,1,0:T(8,128)S(1)}, u32[]{:S(2)}, u32[]{:S(2)}) collective-permute-start(f32[17,8,128]{2,1,0:T(8,128)S(1)} %get-tuple-element.85), channel_id=1, source_target_pairs={{0,12},{1,0},{2,4},{3,8},{4,14},{5,2},{6,6},{7,10},{8,13},{9,1},{1... | collective-permute-start | bytes 208904 | tf_op jit(solution)/shard_map/ppermute | solution.py:519
  9.8 3.4 %collective-permute-start.2 = (f32[17,8,128]{2,1,0:T(8,128)S(1)}, f32[17,8,128]{2,1,0:T(8,128)S(1)}, u32[]{:S(2)}, u32[]{:S(2)}) collective-permute-start(f32[17,8,128]{2,1,0:T(8,128)S(1)} %get-tuple-element.83), channel_id=1, source_target_pairs={{0,4},{1,8},{2,12},{3,0},{4,6},{5,10},{6,14},{7,2},{8,5},{9,9},{10... | collective-permute-start | bytes 208904 | tf_op jit(solution)/shard_map/ppermute | solution.py:519
  14.2 1.3 collective-permute-done.2
  15.6 5.8 %collective-permute-start.4 = (f32[4,9,8,128]{3,2,1,0:T(8,128)S(1)}, f32[4,9,8,128]{3,2,1,0:T(8,128)S(1)}, u32[]{:S(2)}, u32[]{:S(2)}) collective-permute-start(f32[4,9,8,128]{3,2,1,0:T(8,128)S(1)} %constant_dynamic-slice_fusion.1), channel_id=1, source_target_pairs={{0,2},{1,3},{2,0},{3,1},{4,6},{5,7},{6,4},{7,5},{8,10},{9,11},{10,... | collective-permute-start | bytes 442376 | tf_op jit(solution)/shard_map/ppermute | solution.py:531
  24.7 1.9 %pad_maximum_fusion.5.refs_1_ = f32[4]{0:T(128)} fusion(f32[1]{0:T(128)} %bitcast.20, f32[1]{0:T(128)} %bitcast.19, f32[1]{0:T(128)} %bitcast.18, f32[1]{0:T(128)} %bitcast.17), kind=kLoop, calls=%fused_computation.69 | loop fusion | flops 12 | bytes 32 | tf_op jit(solution)/shard_map/stack | solution.py:498
  27.3 1.2 collective-permute-done.5.refs_3_
  29.7 5.4 %force_0.1 = (f32[64,8,128]{2,1,0:T(8,128)S(1)}, f32[64,8,128]{2,1,0:T(8,128)S(1)}, f32[8,8,128]{2,1,0:T(8,128)S(1)}, f32[9,8,128]{2,1,0:T(8,128)S(1)}) custom-call(s32[818]{0:T(1024)} %concatenate.33.refs_0_, f32[4]{0:T(128)} %pad_maximum_fusion.5.refs_1_, f32[64,8,128]{2,1,0:T(8,128)S(1)} %bitcast.107, f32[9,8,128]{2,1,0:T(8,128)S(1)} %collective-permute-done.5.refs_3_), custom_call_target="tpu_custom_call" | custom-call | tf_op jit(solution)/shard_map/force_0/pallas_call | solution.py:460
  36.9 5.5 %force_1.1 = (f32[64,8,128]{2,1,0:T(8,128)S(1)}, f32[64,8,128]{2,1,0:T(8,128)S(1)}, f32[8,8,128]{2,1,0:T(8,128)S(1)}, f32[9,8,128]{2,1,0:T(8,128)S(1)}) custom-call(s32[818]{0:T(1024)} %concatenate.33.refs_0_, f32[4]{0:T(128)} %pad_maximum_fusion.5.refs_1_, f32[64,8,128]{2,1,0:T(8,128)S(1)} %get-tuple-element.38.refs_2_, ...), custom_call_target="tpu_custom_call" | custom-call | tf_op jit(solution)/shard_map/force_1/pallas_call | solution.py:460
  42.6 1.1 collective-permute-done.8.refs_3_.refs_7_
  43.7 5.6 %force_2.1 = (f32[64,8,128]{2,1,0:T(8,128)S(1)}, f32[64,8,128]{2,1,0:T(8,128)S(1)}, f32[8,8,128]{2,1,0:T(8,128)S(1)}, f32[9,8,128]{2,1,0:T(8,128)S(1)}, f32[8,128]{1,0:T(8,128)S(1)}) custom-call(s32[818]{0:T(1024)} %concatenate.33.refs_0_, f32[4]{0:T(128)} %pad_maximum_fusion.5.refs_1_, f32[64,8,128]{2,1,0:T(8,128)S(1)} %get-tuple-element.42.refs_2_.refs_9_, ...), custom_call_target="tpu_custom_call" | custom-call | tf_op jit(solution)/shard_map/force_2/pallas_call | solution.py:460
  50.6 5.6 %force_3.1 = (f32[64,8,128]{2,1,0:T(8,128)S(1)}, f32[64,8,128]{2,1,0:T(8,128)S(1)}, f32[8,8,128]{2,1,0:T(8,128)S(1)}, f32[9,8,128]{2,1,0:T(8,128)S(1)}, f32[8,128]{1,0:T(8,128)S(1)}) custom-call(s32[818]{0:T(1024)} %concatenate.33.refs_0_, f32[4]{0:T(128)} %pad_maximum_fusion.5.refs_1_, f32[64,8,128]{2,1,0:T(8,128)S(1)} %get-tuple-element.46.refs_2_.refs_9_, ...), custom_call_target="tpu_custom_call" | custom-call | tf_op jit(solution)/shard_map/force_3/pallas_call | solution.py:460
  57.7 6.4 %force_4.1 = (f32[64,8,128]{2,1,0:T(8,128)S(1)}, f32[64,8,128]{2,1,0:T(8,128)}, f32[8,8,128]{2,1,0:T(8,128)S(1)}, f32[9,8,128]{2,1,0:T(8,128)S(1)}, f32[8,128]{1,0:T(8,128)S(1)}) custom-call(s32[818]{0:T(1024)} %concatenate.33.refs_0_, f32[4]{0:T(128)} %pad_maximum_fusion.5.refs_1_, f32[64,8,128]{2,1,0:T(8,128)S(1)} %get-tuple-element.50.refs_2_.refs_7_, ...), custom_call_target="tpu_custom_call" | custom-call | tf_op jit(solution)/shard_map/force_4/pallas_call | solution.py:460
  64.2 1.1 collective-permute-done.12.refs_5_
  65.3 13.2 %adjoint_4.1 = (f32[64,8,128]{2,1,0:T(8,128)S(1)}, f32[9,8,128]{2,1,0:T(8,128)S(1)}, f32[64,8,128]{2,1,0:T(8,128)S(1)}) custom-call(s32[818]{0:T(1024)} %concatenate.33.refs_0_, f32[4]{0:T(128)} %pad_maximum_fusion.5.refs_1_, f32[64,8,128]{2,1,0:T(8,128)S(1)} %get-tuple-element.55.refs_2_, f32[8,8,128]{2,1,0:T(8,128)S(1)} %get-tuple-element.56.refs_3_, ...), custom_call_target="tpu_custom_call" | custom-call | tf_op jit(solution)/shard_map/adjoint_4/pallas_call | solution.py:460
  79.8 13.4 %adjoint_3.1 = (f32[64,8,128]{2,1,0:T(8,128)S(1)}, f32[9,8,128]{2,1,0:T(8,128)S(1)}) custom-call(s32[818]{0:T(1024)} %concatenate.33.refs_0_, f32[4]{0:T(128)} %pad_maximum_fusion.5.refs_1_, f32[64,8,128]{2,1,0:T(8,128)S(1)} %get-tuple-element.50.refs_2_.refs_7_, f32[8,8,128]{2,1,0:T(8,128)S(1)} %get-tuple-element.51.refs_3_, ...), custom_call_target="tpu_custom_call" | custom-call | tf_op jit(solution)/shard_map/adjoint_3/pallas_call | solution.py:460
  94.5 13.4 %adjoint_2.1 = (f32[64,8,128]{2,1,0:T(8,128)S(1)}, f32[9,8,128]{2,1,0:T(8,128)S(1)}) custom-call(s32[818]{0:T(1024)} %concatenate.33.refs_0_, f32[4]{0:T(128)} %pad_maximum_fusion.5.refs_1_, f32[64,8,128]{2,1,0:T(8,128)S(1)} %get-tuple-element.46.refs_2_.refs_9_, f32[8,8,128]{2,1,0:T(8,128)S(1)} %get-tuple-element.47.refs_3_, ...), custom_call_target="tpu_custom_call" | custom-call | tf_op jit(solution)/shard_map/adjoint_2/pallas_call | solution.py:460
  109.2 13.3 %adjoint_1.1 = (f32[64,8,128]{2,1,0:T(8,128)S(1)}, f32[9,8,128]{2,1,0:T(8,128)S(1)}) custom-call(s32[818]{0:T(1024)} %concatenate.33.refs_0_, f32[4]{0:T(128)} %pad_maximum_fusion.5.refs_1_, f32[64,8,128]{2,1,0:T(8,128)S(1)} %get-tuple-element.42.refs_2_.refs_9_, f32[8,8,128]{2,1,0:T(8,128)S(1)} %get-tuple-element.43.refs_3_, ...), custom_call_target="tpu_custom_call" | custom-call | tf_op jit(solution)/shard_map/adjoint_1/pallas_call | solution.py:460
  123.9 12.9 %adjoint_0.1 = f32[64,16,128]{2,1,0:T(8,128)S(1)} custom-call(s32[818]{0:T(1024)} %concatenate.33.refs_0_, f32[4]{0:T(128)} %pad_maximum_fusion.5.refs_1_, f32[64,8,128]{2,1,0:T(8,128)S(1)} %get-tuple-element.38.refs_2_, f32[8,8,128]{2,1,0:T(8,128)S(1)} %get-tuple-element.39.refs_3_, f32[64,8,128]{2,1,0:T(8,128)S(1)} %get-tuple-element.67.refs_4_, ...), custom_call_target="tpu_custom_call" | custom-call | tf_op jit(solution)/shard_map/adjoint_0/pallas_call | solution.py:460
  137.5 5.6 %collective-permute-start.18 = (f32[8,16,128]{2,1,0:T(8,128)S(1)}, f32[8,16,128]{2,1,0:T(8,128)S(1)}, u32[]{:S(2)}, u32[]{:S(2)}) collective-permute-start(f32[8,16,128]{2,1,0:T(8,128)S(1)} %get-tuple-element.78), channel_id=1, source_target_pairs={{4,0},{8,1},{12,2},{0,3},{6,4},{10,5},{14,6},{2,7},{5,8},{9,9},{13... | collective-permute-start | bytes 196616 | tf_op jit(solution)/shard_map/ppermute | solution.py:641
  143.1 1.3 collective-permute-start.19
  144.5 3.8 %collective-permute-start.20 = (f32[8,16,128]{2,1,0:T(8,128)S(1)}, f32[8,16,128]{2,1,0:T(8,128)S(1)}, u32[]{:S(2)}, u32[]{:S(2)}) collective-permute-start(f32[8,16,128]{2,1,0:T(8,128)S(1)} %get-tuple-element.76), channel_id=1, source_target_pairs={{12,0},{0,1},{4,2},{8,3},{14,4},{2,5},{6,6},{10,7},{13,8},{1,9},{5... | collective-permute-start | bytes 196616 | tf_op jit(solution)/shard_map/ppermute | solution.py:641
  148.3 4.7 %collective-permute-done.20 = f32[8,16,128]{2,1,0:T(8,128)S(1)} collective-permute-done((f32[8,16,128]{2,1,0:T(8,128)S(1)}, f32[8,16,128]{2,1,0:T(8,128)S(1)}, u32[]{:S(2)}, u32[]{:S(2)}) %collective-permute-start.20) | collective-permute-done | bytes 65568 | tf_op jit(solution)/shard_map/ppermute | solution.py:641
  153.8 10.8 %all-to-all-start = ((f32[16,1,1024]{2,1,0:T(1,128)}), f32[16,1,1024]{2,1,0:T(1,128)S(1)}, u32[]{:S(2)}, u32[]{:S(2)}) async-start(f32[16,1,1024]{2,1,0:T(1,128)} %broadcast_in_dim.96), calls=%async_computation | async-start | bytes 131072 | tf_op jit(solution)/shard_map/all_to_all | solution.py:657
  167.8 5.8 %all-to-all-done = f32[16,1,1024]{2,1,0:T(1,128)S(1)} async-done(((f32[16,1,1024]{2,1,0:T(1,128)}), f32[16,1,1024]{2,1,0:T(1,128)S(1)}, u32[]{:S(2)}, u32[]{:S(2)}) %all-to-all-start) | async-done | bytes 65568 | tf_op jit(solution)/shard_map/all_to_all | solution.py:657
  (125 shorter events, 21.8 us)
Async XLA Ops:
  3.7 10.5 %collective-permute-start = (f32[17,8,128]{2,1,0:T(8,128)S(1)}, f32[17,8,128]{2,1,0:T(8,128)S(1)}, u32[]{:S(2)}, u32[]{:S(2)}) collective-permute-start(f32[17,8,128]{2,1,0:T(8,128)S(1)} %get-tuple-element.85), channel_id=1, source_target_pairs={{0,12},{1,0},{2,4},{3,8},{4,14},{5,2},{6,6},{7,10},{8,13},{9,1},{1... | collective-permute-start | bytes 208904 | tf_op jit(solution)/shard_map/ppermute | solution.py:519
  9.7 4.5 %collective-permute-start.1 = (f32[17,8,128]{2,1,0:T(8,128)S(1)}, f32[17,8,128]{2,1,0:T(8,128)S(1)}, u32[]{:S(2)}, u32[]{:S(2)}) collective-permute-start(f32[17,8,128]{2,1,0:T(8,128)S(1)} %get-tuple-element.84), channel_id=1, source_target_pairs={{0,8},{1,12},{2,0},{3,4},{4,10},{5,14},{6,2},{7,6},{8,9},{9,13},{1... | collective-permute-start | bytes 208904 | tf_op jit(solution)/shard_map/ppermute | solution.py:519
  9.8 4.1 %copy-start.7 = (f32[4]{0:T(128)S(1)}, f32[4]{0:T(128)}, u32[]{:S(2)}) copy-start(f32[4]{0:T(128)} %param.15) | copy-start | bytes 52
  9.8 5.6 %collective-permute-start.2 = (f32[17,8,128]{2,1,0:T(8,128)S(1)}, f32[17,8,128]{2,1,0:T(8,128)S(1)}, u32[]{:S(2)}, u32[]{:S(2)}) collective-permute-start(f32[17,8,128]{2,1,0:T(8,128)S(1)} %get-tuple-element.83), channel_id=1, source_target_pairs={{0,4},{1,8},{2,12},{3,0},{4,6},{5,10},{6,14},{7,2},{8,5},{9,9},{10... | collective-permute-start | bytes 208904 | tf_op jit(solution)/shard_map/ppermute | solution.py:519
  13.3 2.2 %collective-permute-start.3 = (f32[17,8,128]{2,1,0:T(8,128)S(1)}, f32[17,8,128]{2,1,0:T(8,128)S(1)}, u32[]{:S(2)}, u32[]{:S(2)}) collective-permute-start(f32[17,8,128]{2,1,0:T(8,128)S(1)} %get-tuple-element.82), channel_id=1, source_target_pairs={{0,0},{1,4},{2,8},{3,12},{4,2},{5,6},{6,10},{7,14},{8,1},{9,5},{10... | collective-permute-start | bytes 208904 | tf_op jit(solution)/shard_map/ppermute | solution.py:519
  14.0 7.4 %collective-permute-start.6 = (f32[4]{0:T(128)S(1)}, f32[4]{0:T(128)S(1)}, u32[]{:S(2)}, u32[]{:S(2)}) collective-permute-start(f32[4]{0:T(128)S(1)} %copy-done.7), channel_id=1, source_target_pairs={{0,16},{16,0},{32,48},{48,32},{64,80},{80,64},{96,112},{112,96},{1... | collective-permute-start | bytes 56 | tf_op jit(solution)/shard_map/ppermute | solution.py:493
  15.6 5.8 %copy-start.8 = (s32[4]{0:T(128)S(1)}, s32[4]{0:T(128)}, u32[]{:S(2)}) copy-start(s32[4]{0:T(128)} %param.16) | copy-start | bytes 52
  15.6 11.0 %collective-permute-start.4 = (f32[4,9,8,128]{3,2,1,0:T(8,128)S(1)}, f32[4,9,8,128]{3,2,1,0:T(8,128)S(1)}, u32[]{:S(2)}, u32[]{:S(2)}) collective-permute-start(f32[4,9,8,128]{3,2,1,0:T(8,128)S(1)} %constant_dynamic-slice_fusion.1), channel_id=1, source_target_pairs={{0,2},{1,3},{2,0},{3,1},{4,6},{5,7},{6,4},{7,5},{8,10},{9,11},{10,... | collective-permute-start | bytes 442376 | tf_op jit(solution)/shard_map/ppermute | solution.py:531
  27.2 1.3 collective-permute-start.5
  35.1 1.3 collective-permute-start.7
  36.4 20.2 %collective-permute-start.11 = (f32[4,8,8,128]{3,2,1,0:T(8,128)S(1)}, f32[4,8,8,128]{3,2,1,0:T(8,128)S(1)}, u32[]{:S(2)}, u32[]{:S(2)}) collective-permute-start(f32[4,8,8,128]{3,2,1,0:T(8,128)S(1)} %constant_dynamic-slice_fusion.2), channel_id=1, source_target_pairs={{0,2},{1,3},{2,0},{3,1},{4,6},{5,7},{6,4},{7,5},{8,10},{9,11},{10,... | collective-permute-start | bytes 393224 | tf_op jit(solution)/shard_map/ppermute | solution.py:531
  42.4 1.3 collective-permute-start.8
  49.3 1.3 collective-permute-start.9
  56.2 1.5 collective-permute-start.10
  64.0 1.2 collective-permute-start.12
  78.5 1.3 collective-permute-start.13
  93.2 1.3 collective-permute-start.14
  107.9 1.3 collective-permute-start.15
  122.6 1.3 collective-permute-start.16
  136.8 11.4 %collective-permute-start.17 = (f32[8,16,128]{2,1,0:T(8,128)S(1)}, f32[8,16,128]{2,1,0:T(8,128)S(1)}, u32[]{:S(2)}, u32[]{:S(2)}) collective-permute-start(f32[8,16,128]{2,1,0:T(8,128)S(1)} %get-tuple-element.79), channel_id=1, source_target_pairs={{0,0},{4,1},{8,2},{12,3},{2,4},{6,5},{10,6},{14,7},{1,8},{5,9},{9,... | collective-permute-start | bytes 196616 | tf_op jit(solution)/shard_map/ppermute | solution.py:641
  137.5 10.7 %collective-permute-start.18 = (f32[8,16,128]{2,1,0:T(8,128)S(1)}, f32[8,16,128]{2,1,0:T(8,128)S(1)}, u32[]{:S(2)}, u32[]{:S(2)}) collective-permute-start(f32[8,16,128]{2,1,0:T(8,128)S(1)} %get-tuple-element.78), channel_id=1, source_target_pairs={{4,0},{8,1},{12,2},{0,3},{6,4},{10,5},{14,6},{2,7},{5,8},{9,9},{13... | collective-permute-start | bytes 196616 | tf_op jit(solution)/shard_map/ppermute | solution.py:641
  143.1 5.2 %collective-permute-start.19 = (f32[8,16,128]{2,1,0:T(8,128)S(1)}, f32[8,16,128]{2,1,0:T(8,128)S(1)}, u32[]{:S(2)}, u32[]{:S(2)}) collective-permute-start(f32[8,16,128]{2,1,0:T(8,128)S(1)} %get-tuple-element.77), channel_id=1, source_target_pairs={{8,0},{12,1},{0,2},{4,3},{10,4},{14,5},{2,6},{6,7},{9,8},{13,9},{1... | collective-permute-start | bytes 196616 | tf_op jit(solution)/shard_map/ppermute | solution.py:641
  144.5 8.6 %collective-permute-start.20 = (f32[8,16,128]{2,1,0:T(8,128)S(1)}, f32[8,16,128]{2,1,0:T(8,128)S(1)}, u32[]{:S(2)}, u32[]{:S(2)}) collective-permute-start(f32[8,16,128]{2,1,0:T(8,128)S(1)} %get-tuple-element.76), channel_id=1, source_target_pairs={{12,0},{0,1},{4,2},{8,3},{14,4},{2,5},{6,6},{10,7},{13,8},{1,9},{5... | collective-permute-start | bytes 196616 | tf_op jit(solution)/shard_map/ppermute | solution.py:641
  153.8 19.9 %all-to-all-start = ((f32[16,1,1024]{2,1,0:T(1,128)}), f32[16,1,1024]{2,1,0:T(1,128)S(1)}, u32[]{:S(2)}, u32[]{:S(2)}) async-start(f32[16,1,1024]{2,1,0:T(1,128)} %broadcast_in_dim.96), calls=%async_computation | async-start | bytes 131072 | tf_op jit(solution)/shard_map/all_to_all | solution.py:657
  (7 other events, 5.3 us)
